TPU v7x, 128 devices: a whole 4x4x4 slice. The times are simulated.
128 devices in a mesh: data: 1, sp: 128 (over z, y, x, core).
Axes of the slice: x: 4, y: 4, z: 4, core: 2. Of those that a mesh axis runs over, the one named last changes fastest.
Arguments:
- latent: bfloat16 [1, 768, 1024, 384], P('data', 'sp')
- ln_gain: bfloat16 [4, 384], replicated
- ln_bias: bfloat16 [4, 384], replicated
- w_qkv: bfloat16 [2, 384, 3, 6, 64], replicated
- w_out: bfloat16 [2, 6, 64, 384], replicated
- w_up: bfloat16 [2, 384, 1536], replicated
- w_down: bfloat16 [2, 1536, 384], replicated
Outputs:
- output: bfloat16 [1, 768, 1024, 384], P('data', 'sp')
All inputs are finite; a program needn't handle non-finite values.
Results may differ from a plain program's by a relative error of at most 0.0106958.
Values are sent between devices in bfloat16 or wider.
A program may use at most 1 GiB of HBM per device.

v0:
```python
import jax
import jax.numpy as jnp
from jax import lax
from jax.sharding import PartitionSpec as P, NamedSharding

LN_EPS = 1e-6
SPACE_FORMS = ('btqhk,btphk->bthqp', 'bthqp,btphk->btqhk')
TIME_FORMS = ('bqshk,bpshk->bshqp', 'bshqp,bpshk->bqshk')


def layer_norm(tokens, gain_vec, shift_vec):
    as_float = tokens.astype(jnp.float32)
    mean_val = jnp.mean(as_float, axis=-1, keepdims=True)
    centered = as_float - mean_val
    variance = jnp.mean(centered * centered, axis=-1, keepdims=True)
    normed = centered * lax.rsqrt(variance + LN_EPS) * gain_vec.astype(jnp.float32) + shift_vec.astype(jnp.float32)
    return normed.astype(jnp.bfloat16)


def project_qkv(tokens, gain_vec, shift_vec, w_qkv_blk):
    normed = layer_norm(tokens, gain_vec, shift_vec)
    return jnp.einsum('btsd,dchk->btschk', normed, w_qkv_blk, preferred_element_type=jnp.float32).astype(jnp.bfloat16)


def attend(qkv_all, ein_forms):
    score_scale = qkv_all.shape[-1] ** -0.5
    query_rows = qkv_all[:, :, :, 0]
    key_rows = qkv_all[:, :, :, 1]
    value_rows = qkv_all[:, :, :, 2]
    scores = jnp.einsum(ein_forms[0], query_rows, key_rows, preferred_element_type=jnp.float32) * score_scale
    attn_probs = jax.nn.softmax(scores, axis=-1).astype(jnp.bfloat16)
    return jnp.einsum(ein_forms[1], attn_probs, value_rows, preferred_element_type=jnp.float32).astype(jnp.bfloat16)


def finish_block(tokens, attended, gain_vec, shift_vec, w_out_blk, w_up_blk, w_down_blk):
    projected = jnp.einsum('btshk,hkd->btsd', attended, w_out_blk, preferred_element_type=jnp.float32)
    residual = (tokens.astype(jnp.float32) + projected).astype(jnp.bfloat16)
    normed = layer_norm(residual, gain_vec, shift_vec)
    hidden = jax.nn.gelu(jnp.einsum('btsd,df->btsf', normed, w_up_blk, preferred_element_type=jnp.float32), approximate=True).astype(jnp.bfloat16)
    result = residual.astype(jnp.float32) + jnp.einsum('btsf,fd->btsd', hidden, w_down_blk, preferred_element_type=jnp.float32)
    return result.astype(jnp.bfloat16)


def value_a9(tokens, layer_idx, ein_forms, ln_gain, ln_bias, w_qkv, w_out, w_up, w_down):
    qkv_all = project_qkv(tokens, ln_gain[2 * layer_idx], ln_bias[2 * layer_idx], w_qkv[layer_idx])
    attended = attend(qkv_all, ein_forms)
    return finish_block(tokens, attended, ln_gain[2 * layer_idx + 1], ln_bias[2 * layer_idx + 1], w_out[layer_idx], w_up[layer_idx], w_down[layer_idx])


def solution(mesh):
    act_spec = P('data', 'sp', None, None)

    def local_run(local_latent, ln_gain, ln_bias, w_qkv, w_out, w_up, w_down):
        mixed_act = value_a9(local_latent, 0, SPACE_FORMS, ln_gain, ln_bias, w_qkv, w_out, w_up, w_down)
        mixed_act = lax.all_to_all(mixed_act, 'sp', 2, 1, tiled=True)
        mixed_act = value_a9(mixed_act, 1, TIME_FORMS, ln_gain, ln_bias, w_qkv, w_out, w_up, w_down)
        return lax.all_to_all(mixed_act, 'sp', 1, 2, tiled=True)

    return jax.shard_map(local_run, mesh=mesh, in_specs=(act_spec, P(), P(), P(), P(), P(), P()), out_specs=act_spec, check_vma=False)
```

profile of v0, /device:TPU:1, one launch (start us, length us, event | category | flops | bytes accessed | tf_op | source)
XLA Modules:
  0.0 520.0 jit_solution(7467292002833058702)
XLA Ops:
  0.0 6.7 %copy.48 = bf16[1,6,1024,384]{2,3,1,0:T(8,128)(2,1)} copy(bf16[1,6,1024,384]{3,2,1,0:T(8,128)(2,1)} %param.7) | data formatting | bytes 9437184 | tf_op args[0]
  6.8 3.5 convert_reduce_fusion.2
  10.3 3.6 fusion.48
  14.0 0.6 convert_reduce_fusion.3
  14.6 10.7 %convert_bitcast_fusion.1 = bf16[1,6,1024,3,6,64]{2,5,4,3,1,0:T(8,128)(2,1)} fusion(bf16[1,6,1024,384]{2,3,1,0:T(8,128)(2,1)S(1)} %copy-done, f32[384]{0:T(512)S(1)} %get-tuple-element.11, f32[384]{0:T(512)S(1)} %get-tuple-element.22, f32[6,1024]{1,0:T(8,128)S(1)} %add_rsqrt_fusion.2, f32[6,1024]{1,0:T(8,128)S(1)} %broadcast_multiply_fusion.2, ...), kind=kOutput, calls=%fused_computation.36 | convolution fusion | flops 5457051648 | bytes 19828736 | tf_op jit(solution)/shard_map/btsd,dchk->btschk/dot_general | solution.py:22
  25.3 57.5 %fusion.146 = (f32[6,6,1024]{2,1,0:T(8,128)S(1)}, f32[6,6,1024,1024]{2,3,1,0:T(8,128)}) fusion(bf16[1,6,1024,3,6,64]{2,5,4,3,1,0:T(8,128)(2,1)} %convert_bitcast_fusion.1), kind=kOutput, calls=%fused_computation.149 | convolution fusion | flops 4945085440 | bytes 160579584 | tf_op jit(solution)/shard_map/sub | solution.py:31
  82.9 50.1 %fusion.115.clone.5 = bf16[6,1024,6,64]{1,3,2,0:T(8,128)(2,1)} fusion(f32[6,6,1024,1024]{2,3,1,0:T(8,128)} %get-tuple-element.14, f32[6,6,1024]{2,1,0:T(8,128)S(1)} %get-tuple-element.13, bf16[1,6,1024,3,6,64]{2,5,4,3,1,0:T(8,128)(2,1)} %convert_bitcast_fusion.1), kind=kOutput, calls=%fused_computation.88.clone.clone.clone.clone.clone.2 | convolution fusion | flops 4909694976 | bytes 160579584 | tf_op jit(solution)/shard_map/bthqp,btphk->btqhk/dot_general | solution.py:32
  133.0 0.0 copy-start.13
  133.0 7.4 %convert_reduce_fusion.1 = (f32[6,1024]{1,0:T(8,128)S(1)}, bf16[1,6,1024,384]{2,3,1,0:T(8,128)(2,1)S(1)}) fusion(bf16[2,6,64,384]{3,2,1,0:T(8,128)(2,1)S(1)} %copy-done.3, bf16[1,6,1024,384]{2,3,1,0:T(8,128)(2,1)} %copy.48, bf16[6,1024,6,64]{1,3,2,0:T(8,128)(2,1)} %fusion.115.clone.5), kind=kOutput, calls=%fused_computation.42 | convolution fusion | flops 1823729664 | bytes 14475264 | tf_op jit(solution)/shard_map/btshk,hkd->btsd/dot_general | solution.py:36
  140.5 2.2 copy-done.2
  142.6 1.3 fusion.44
  144.0 28.0 %fusion.53 = bf16[1,6,1024,384]{2,3,1,0:T(8,128)(2,1)} fusion(bf16[1,6,1024,384]{2,3,1,0:T(8,128)(2,1)} %copy-done.2, f32[384]{0:T(512)S(1)} %copy-done.11, f32[384]{0:T(512)S(1)} %copy-done.12, f32[6,1024]{1,0:T(8,128)S(1)} %add_rsqrt_fusion.1, f32[6,1024]{1,0:T(8,128)S(1)} %broadcast_multiply_fusion.1, bf16[2,1536,384]{2,1,0:T(8,128)(2,1)S(1)} %copy-done.13, ...), kind=kOutput, calls=%fused_computation.65 | convolution fusion | flops 14601682944 | bytes 16584704 | tf_op jit(solution)/shard_map/btsf,fd->btsd/dot_general | solution.py:40
  172.0 8.5 %copy.53 = bf16[1,6,1024,384]{3,1,0,2:T(8,128)(2,1)} copy(bf16[1,6,1024,384]{2,3,1,0:T(8,128)(2,1)} %fusion.53) | data formatting | bytes 9437184 | tf_op jit(solution)/shard_map/convert_element_type | solution.py:41
  180.5 96.9 %all_to_all.27 = bf16[1,6,1024,384]{3,1,0,2:T(8,128)(2,1)S(1)} all-to-all(bf16[1,6,1024,384]{3,1,0,2:T(8,128)(2,1)} %copy.53), channel_id=1, replica_groups=mesh['data'=1,'sp'=128] {'sp'}, dimensions={2} | all-to-all | bytes 9437184 | tf_op jit(solution)/shard_map/all_to_all | solution.py:55
  277.4 1.3 fusion.58
  278.7 2.7 multiply_reduce_fusion.2
  281.4 0.1 add_rsqrt_fusion
  281.5 2.2 add_convert_fusion
  283.7 2.7 copy.56
  286.4 0.6 convert_bitcast_fusion.2
  287.0 4.4 copy.55
  291.4 9.9 %copy.59 = f32[768,8,384]{0,2,1:T(8,128)} copy(f32[768,8,384]{2,1,0:T(8,128)} %bitcast.207) | data formatting | bytes 18874368 | tf_op jit(solution)/shard_map/convert_element_type | solution.py:37
  301.2 13.1 %convert_bitcast_fusion = bf16[1,768,8,3,6,64]{1,5,4,3,2,0:T(8,128)(2,1)} fusion(bf16[768,8,384,1,1]{2,1,0,4,3:T(8,128)(2,1)} %bitcast.209, bf16[2,384,3,6,64]{1,4,3,2,0:T(8,128)(2,1)S(1)} %copy-done.16), kind=kOutput, calls=%fused_computation.35 | convolution fusion | flops 5442895872 | bytes 19759104 | tf_op jit(solution)/shard_map/btsd,dchk->btschk/dot_general | solution.py:22
  314.3 43.3 %fusion.147 = (f32[8,6,768]{2,1,0:T(8,128)S(1)}, f32[8,6,768,768]{2,3,1,0:T(8,128)}) fusion(bf16[1,768,8,3,6,64]{1,5,4,3,2,0:T(8,128)(2,1)} %convert_bitcast_fusion), kind=kOutput, calls=%fused_computation.150 | convolution fusion | flops 3708814080 | bytes 122830848 | tf_op jit(solution)/shard_map/sub | solution.py:31
  357.6 39.1 %fusion.113.clone.5 = bf16[768,8,6,64]{0,3,2,1:T(8,128)(2,1)} fusion(f32[8,6,768,768]{2,3,1,0:T(8,128)} %get-tuple-element.18, f32[8,6,768]{2,1,0:T(8,128)S(1)} %get-tuple-element.17, bf16[1,768,8,3,6,64]{1,5,4,3,2,0:T(8,128)(2,1)} %convert_bitcast_fusion), kind=kOutput, calls=%fused_computation.86.clone.clone.clone.clone.clone.2 | convolution fusion | flops 3682861056 | bytes 122830848 | tf_op jit(solution)/shard_map/bshqp,bpshk->bqshk/dot_general | solution.py:32
  396.7 8.1 %convert_reduce_fusion = (f32[768,8]{0,1:T(8,128)S(1)}, bf16[768,8,384]{0,2,1:T(8,128)(2,1)S(1)}) fusion(f32[768,8,384]{0,2,1:T(8,128)} %copy.59, bf16[2,6,64,384]{3,2,1,0:T(8,128)(2,1)S(1)} %copy-done.4, bf16[768,8,6,64]{0,3,2,1:T(8,128)(2,1)} %fusion.113.clone.5), kind=kOutput, calls=%fused_computation.39 | convolution fusion | flops 1821370368 | bytes 19193856 | tf_op jit(solution)/shard_map/btshk,hkd->btsd/dot_general | solution.py:36
  404.8 2.2 copy-done.1
  407.0 1.3 fusion.40
  408.3 27.2 %fusion.59 = bf16[1,768,8,384]{1,3,2,0:T(8,128)(2,1)} fusion(bf16[768,8,384]{0,2,1:T(8,128)(2,1)} %copy-done.1, f32[384]{0:T(512)S(1)} %copy-done.9, f32[384]{0:T(512)S(1)} %copy-done.10, f32[768,8]{0,1:T(8,128)S(1)} %add_rsqrt_fusion.3, f32[768,8]{0,1:T(8,128)S(1)} %broadcast_multiply_fusion.3, bf16[2,1536,384]{2,1,0:T(8,128)(2,1)S(1)} %copy-done.14, ...), kind=kOutput, calls=%fused_computation.74 | convolution fusion | flops 14601682944 | bytes 16568320 | tf_op jit(solution)/shard_map/btsf,fd->btsd/dot_general | solution.py:40
  435.5 7.0 %copy.62 = bf16[1,768,8,384]{3,2,0,1:T(8,128)(2,1)} copy(bf16[1,768,8,384]{1,3,2,0:T(8,128)(2,1)} %fusion.59) | data formatting | bytes 9437184 | tf_op jit(solution)/shard_map/convert_element_type | solution.py:41
  442.5 74.3 %all_to_all.28 = bf16[1,768,8,384]{3,2,0,1:T(8,128)(2,1)S(1)} all-to-all(bf16[1,768,8,384]{3,2,0,1:T(8,128)(2,1)} %copy.62), channel_id=1, replica_groups=mesh['data'=1,'sp'=128] {'sp'}, dimensions={1} | all-to-all | bytes 9437184 | tf_op jit(solution)/shard_map/all_to_all | solution.py:57
  516.8 2.7 copy.85
  (38 shorter events, 0.2 us)
Async XLA Ops:
  0.0 13.9 %copy-start.5 = (bf16[4,384]{1,0:T(4,128)(2,1)S(1)}, bf16[4,384]{1,0:T(4,128)(2,1)}, u32[]{:S(2)}) copy-start(bf16[4,384]{1,0:T(4,128)(2,1)} %param.9) | copy-start | bytes 9220
  0.0 14.0 %copy-start.6 = (bf16[4,384]{1,0:T(4,128)(2,1)S(1)}, bf16[4,384]{1,0:T(4,128)(2,1)}, u32[]{:S(2)}) copy-start(bf16[4,384]{1,0:T(4,128)(2,1)} %param.8) | copy-start | bytes 9220
  0.0 14.6 %copy-start.15 = (bf16[2,384,3,6,64]{1,4,3,2,0:T(8,128)(2,1)S(1)}, bf16[2,384,3,6,64]{1,4,3,2,0:T(8,128)(2,1)}, u32[]{:S(2)}) copy-start(bf16[2,384,3,6,64]{1,4,3,2,0:T(8,128)(2,1)} %param.10) | copy-start | bytes 5308420
  6.8 7.9 %copy-start = (bf16[1,6,1024,384]{2,3,1,0:T(8,128)(2,1)S(1)}, bf16[1,6,1024,384]{2,3,1,0:T(8,128)(2,1)}, u32[]{:S(2)}) copy-start(bf16[1,6,1024,384]{2,3,1,0:T(8,128)(2,1)} %copy.48) | copy-start | bytes 14155780
  82.8 50.1 %copy-start.3 = (bf16[2,6,64,384]{3,2,1,0:T(8,128)(2,1)S(1)}, bf16[2,6,64,384]{3,2,1,0:T(8,128)(2,1)}, u32[]{:S(2)}) copy-start(bf16[2,6,64,384]{3,2,1,0:T(8,128)(2,1)} %param.11) | copy-start | bytes 1769476
  133.0 10.9 %copy-start.11 = (f32[384]{0:T(512)S(1)}, f32[384]{0:T(512)}, u32[]{:S(2)}) copy-start(f32[384]{0:T(512)} %get-tuple-element.10) | copy-start | bytes 4612
  133.0 10.9 %copy-start.12 = (f32[384]{0:T(512)S(1)}, f32[384]{0:T(512)}, u32[]{:S(2)}) copy-start(f32[384]{0:T(512)} %get-tuple-element.23) | copy-start | bytes 4612
  133.0 11.0 %copy-start.13 = (bf16[2,1536,384]{2,1,0:T(8,128)(2,1)S(1)}, bf16[2,1536,384]{2,1,0:T(8,128)(2,1)}, u32[]{:S(2)}) copy-start(bf16[2,1536,384]{2,1,0:T(8,128)(2,1)} %param.13) | copy-start | bytes 7077892
  140.4 2.2 copy-start.2
  277.4 4.1 copy-start.7
  277.4 4.1 copy-start.8
  291.4 9.9 %copy-start.16 = (bf16[2,384,3,6,64]{1,4,3,2,0:T(8,128)(2,1)S(1)}, bf16[2,384,3,6,64]{1,4,3,2,0:T(8,128)(2,1)}, u32[]{:S(2)}) copy-start(bf16[2,384,3,6,64]{1,4,3,2,0:T(8,128)(2,1)} %param.10) | copy-start | bytes 5308420
  357.6 39.1 %copy-start.4 = (bf16[2,6,64,384]{3,2,1,0:T(8,128)(2,1)S(1)}, bf16[2,6,64,384]{3,2,1,0:T(8,128)(2,1)}, u32[]{:S(2)}) copy-start(bf16[2,6,64,384]{3,2,1,0:T(8,128)(2,1)} %param.11) | copy-start | bytes 1769476
  396.7 11.6 %copy-start.9 = (f32[384]{0:T(512)S(1)}, f32[384]{0:T(512)}, u32[]{:S(2)}) copy-start(f32[384]{0:T(512)} %get-tuple-element.9) | copy-start | bytes 4612
  396.7 11.6 %copy-start.10 = (f32[384]{0:T(512)S(1)}, f32[384]{0:T(512)}, u32[]{:S(2)}) copy-start(f32[384]{0:T(512)} %get-tuple-element.24) | copy-start | bytes 4612
  396.7 11.6 %copy-start.14 = (bf16[2,1536,384]{2,1,0:T(8,128)(2,1)S(1)}, bf16[2,1536,384]{2,1,0:T(8,128)(2,1)}, u32[]{:S(2)}) copy-start(bf16[2,1536,384]{2,1,0:T(8,128)(2,1)} %param.13) | copy-start | bytes 7077892
  404.8 2.2 copy-start.1
where the time goes:
time: 528 us; the launch traced here: 520 us
  matrix products  285 us (54%)
  blocking collectives  171 us (32%)
  local copies, waits for them, and re-layouts  46.2 us (9%)
  other arithmetic  17.2 us (3%)
    sub x2, matrix products, attend(): attn_probs = jax.nn.softmax(scores, axis=-1).astype(jnp.bfloat16)  101 us
    all_to_all x1, blocking collectives, local_run(): mixed_act = lax.all_to_all(mixed_act, 'sp', 2, 1, tiled=True)  96.9 us
    dot_general x2, matrix products, attend(): jnp.einsum(ein_forms[1], attn_probs, value_rows, preferred_element_type=j...  89.2 us
    all_to_all x1, blocking collectives, local_run(): return lax.all_to_all(mixed_act, 'sp', 1, 2, tiled=True)  74.3 us
    dot_general x2, matrix products, finish_block(): jnp.einsum('btsf,fd->btsd', hidden, w_down_blk, preferred_element_type=jn...  55.3 us
    dot_general x2, matrix products, project_qkv(): jnp.einsum('btsd,dchk->btschk', normed, w_qkv_blk, preferred_element_type...  23.8 us
    convert_element_type x2, local copies, waits for them, and re-layouts, finish_block(): return result.astype(jnp.bfloat16)  15.5 us
    dot_general x2, matrix products, finish_block(): jnp.einsum('btshk,hkd->btsd', attended, w_out_blk, preferred_element_type...  15.5 us

commit v1 on v0

v1 whole, which is shorter than its diff:
```python
import functools
import jax
import jax.numpy as jnp
from jax import lax
from jax.experimental import pallas as pl
from jax.experimental.pallas import tpu as pltpu
from jax.sharding import PartitionSpec as P

LN_EPS = 1e-6
HEADS = 6
HEAD_DIM = 64
BF = jnp.bfloat16
F32 = jnp.float32
SUBL = 8
TILE = 128
CHUNK = 256
EXP2_SCALE = 1.4426950408889634 * HEAD_DIM ** -0.5


def layer_norm(xf, gain, shift):
    mean = jnp.mean(xf, axis=-1, keepdims=True)
    cen = xf - mean
    var = jnp.mean(cen * cen, axis=-1, keepdims=True)
    return (cen * lax.rsqrt(var + LN_EPS) * gain + shift).astype(BF)


def dot(a, b):
    return jnp.dot(a, b, preferred_element_type=F32)


def dot_t(a, b):
    return lax.dot_general(a, b, (((1,), (1,)), ((), ())), preferred_element_type=F32)


def gelu(x):
    inner = x * (0.7978845608028654 + 0.035677408136300125 * (x * x))
    half = 0.5 * x
    return half + half * jnp.tanh(inner)


def attend(q, k_at, v_at):
    lane = lax.broadcasted_iota(jnp.int32, (TILE, 128), 1)
    outs = []
    for pair in range(HEADS // 2):
        qp = q[:, 128 * pair:128 * pair + 128]
        zero = jnp.zeros_like(qp)
        qm = jnp.concatenate([jnp.where(lane < HEAD_DIM, qp, zero), jnp.where(lane < HEAD_DIM, zero, qp)], axis=0)
        s = dot_t(k_at(pair), qm)
        top = jnp.max(s, axis=0, keepdims=True)
        e = jnp.exp2((s - top) * EXP2_SCALE)
        total = jnp.sum(e, axis=0, keepdims=True)
        o = dot(v_at(pair), e.astype(BF)) * (1.0 / total)
        o = jnp.concatenate([o[:HEAD_DIM, :TILE], o[HEAD_DIM:, TILE:]], axis=0)
        outs.append(o.T.astype(BF))
    return jnp.concatenate(outs, axis=1)


def finish(xb, o, gain, shift, wout, wup, wdown):
    h = (xb.astype(F32) + dot(o, wout)).astype(BF)
    hf = h.astype(F32)
    a = layer_norm(hf, gain, shift)
    u = gelu(dot(a, wup)).astype(BF)
    return hf + dot(u, wdown)


def kernel(ndev, frames, x_ref, gain_ref, shift_ref, wqk_ref, wv_ref, wout_ref, wup_ref, wdown_ref, out_ref,
           wvt, qs, ks, vts, os_, sendbuf, recv, xt, q1, k1, v1t, y1, send_sem, recv_sem, loc_sem):
    patches = ndev * SUBL
    width = HEADS * HEAD_DIM
    seq = frames * ndev
    me = lax.axis_index('sp')
    core, cx, cy, cz = me % 2, (me // 2) % 4, (me // 8) % 4, me // 32
    nchunk = patches // CHUNK

    for l in range(2):
        wvt[l] = wv_ref[l].astype(F32).T.astype(BF)

    def peer(i):
        i = (i * 37) % ndev
        dc, dx, dy, dz = i % 2, (i // 2) % 4, (i // 8) % 4, i // 32
        return ((cz + dz) % 4) * 32 + ((cy + dy) % 4) * 8 + ((cx + dx) % 4) * 2 + (core + dc) % 2

    def send_round(stage, dst, j):
        src = sendbuf.at[stage, j]
        own = pltpu.make_async_copy(src.at[me], dst.at[j, me], loc_sem.at[stage, j])
        own.start()

        def body(i, c):
            to = peer(i)
            pltpu.make_async_remote_copy(
                src_ref=src.at[to], dst_ref=dst.at[j, me],
                send_sem=send_sem.at[stage, j], recv_sem=recv_sem.at[stage, j],
                device_id={'sp': to}, device_id_type=pl.DeviceIdType.MESH).start()
            return c
        lax.fori_loop(1, ndev, body, 0)

    def wait_bytes(ref, sem):
        pltpu.make_async_copy(ref, ref, sem).wait()

    def wait_arrived(stage, dst, j):
        pltpu.make_async_copy(sendbuf.at[stage, j, 0], dst.at[j, 0], loc_sem.at[stage, j]).wait()
        wait_bytes(dst.at[j, pl.ds(0, ndev - 1)], recv_sem.at[stage, j])

    def wait_sent(stage, j):
        wait_bytes(sendbuf.at[stage, j, pl.ds(0, ndev - 1)], send_sem.at[stage, j])

    def params(l):
        g = gain_ref[...].astype(F32)
        b = shift_ref[...].astype(F32)
        return g[2 * l:2 * l + 1], b[2 * l:2 * l + 1], g[2 * l + 1:2 * l + 2], b[2 * l + 1:2 * l + 2]

    ga, ba, gm, bm = params(0)

    def frame_step(j, carry):
        def qkv_step(c, cc):
            rows = pl.ds(pl.multiple_of(c * CHUNK, CHUNK), CHUNK)
            a = layer_norm(x_ref[j, rows, :].astype(F32), ga, ba)
            qk = dot(a, wqk_ref[0]).astype(BF)
            qs[rows, :] = qk[:, :width]
            ks[rows, :] = qk[:, width:]
            vts[:, rows] = dot_t(wvt[0], a).astype(BF)
            return cc
        lax.fori_loop(0, nchunk, qkv_step, 0)

        def tile_step(t, cc):
            rows = pl.ds(pl.multiple_of(t * TILE, TILE), TILE)
            os_[rows, :] = attend(qs[rows, :], lambda p: ks[:, 128 * p:128 * p + 128], lambda p: vts[128 * p:128 * p + 128, :])
            return cc
        lax.fori_loop(0, patches // TILE, tile_step, 0)

        def mlp_step(c, cc):
            rows = pl.ds(pl.multiple_of(c * CHUNK, CHUNK), CHUNK)
            y = finish(x_ref[j, rows, :], os_[rows, :], gm, bm, wout_ref[0], wup_ref[0], wdown_ref[0])
            dests = CHUNK // SUBL
            sendbuf[0, j, pl.ds(pl.multiple_of(c * dests, dests), dests)] = y.reshape(dests, SUBL, width).astype(BF)
            return cc
        lax.fori_loop(0, nchunk, mlp_step, 0)
        send_round(0, recv, j)
        return carry
    lax.fori_loop(0, frames, frame_step, 0)

    ga, ba, gm, bm = params(1)
    r_io = lax.broadcasted_iota(jnp.int32, (128, 128), 0)
    c_io = lax.broadcasted_iota(jnp.int32, (128, 128), 1)
    to_seq = jnp.where((r_io // 16 == c_io % 8) & (r_io % 16 == c_io // 8), 1.0, 0.0).astype(BF)
    to_tok = jnp.where((r_io % 8 == c_io // 16) & (r_io // 8 == c_io % 16), 1.0, 0.0).astype(BF)

    def kv_step(j, carry):
        wait_arrived(0, recv, j)

        def perm_step(g, cc):
            blk = recv[j, pl.ds(g * 16, 16)].astype(F32).reshape(128, width).astype(BF)
            seqd = dot(to_seq, blk).astype(BF)
            for p in range(SUBL):
                xt[j, p, pl.ds(pl.multiple_of(g * 16, 16), 16), :] = seqd[16 * p:16 * p + 16]
            return cc
        lax.fori_loop(0, ndev // 16, perm_step, 0)

        def qkv_step(c, cc):
            xb = xt[j, pl.ds(2 * c, 2)].reshape(2 * ndev, width)
            a = layer_norm(xb.astype(F32), ga, ba)
            qk = dot(a, wqk_ref[1]).astype(BF)
            vt = dot_t(wvt[1], a).astype(BF)
            cols = pl.ds(pl.multiple_of(j * ndev, ndev), ndev)
            for i in range(2):
                part = slice(i * ndev, (i + 1) * ndev)
                q1[2 * c + i, cols, :] = qk[part, :width]
                k1[2 * c + i, cols, :] = qk[part, width:]
                v1t[2 * c + i, :, cols] = vt[:, part]
            return cc
        lax.fori_loop(0, SUBL // 2, qkv_step, 0)
        return carry
    lax.fori_loop(0, frames, kv_step, 0)

    def time_step(j, carry):
        cols = pl.ds(pl.multiple_of(j * ndev, ndev), ndev)

        def tile_step(p, cc):
            rows = pl.ds(pl.multiple_of(p * TILE, TILE), TILE)
            os_[rows, :] = attend(q1[p, cols, :], lambda h: k1[p, :, 128 * h:128 * h + 128], lambda h: v1t[p, 128 * h:128 * h + 128, :])
            return cc
        lax.fori_loop(0, SUBL, tile_step, 0)

        def mlp_step(c, cc):
            rows = pl.ds(pl.multiple_of(c * CHUNK, CHUNK), CHUNK)
            y = finish(xt[j, pl.ds(2 * c, 2)].reshape(CHUNK, width), os_[rows, :], gm, bm, wout_ref[1], wup_ref[1], wdown_ref[1])
            y1[pl.ds(2 * c, 2)] = y.astype(BF).reshape(2, ndev, width)
            return cc
        lax.fori_loop(0, SUBL // 2, mlp_step, 0)

        def perm_step(g, cc):
            blk = y1[:, pl.ds(pl.multiple_of(g * 16, 16), 16), :].reshape(128, width)
            tok = dot(to_tok, blk)
            sendbuf[1, j, pl.ds(g * 16, 16)] = tok.reshape(16, SUBL, width).astype(BF)
            return cc
        lax.fori_loop(0, ndev // 16, perm_step, 0)
        send_round(1, out_ref, j)
        return carry
    lax.fori_loop(0, frames, time_step, 0)

    def drain(j, carry):
        wait_sent(0, j)
        wait_sent(1, j)
        wait_arrived(1, out_ref, j)
        return carry
    lax.fori_loop(0, frames, drain, 0)


def solution(mesh):
    ndev = mesh.shape['sp']
    act_spec = P('data', 'sp', None, None)

    def local_run(latent, ln_gain, ln_bias, w_qkv, w_out, w_up, w_down):
        _, frames, patches, width = latent.shape
        wqkv = w_qkv.reshape(2, width, 3 * width)
        wqk, wv = wqkv[:, :, :2 * width], wqkv[:, :, 2 * width:]
        seq = frames * ndev
        out = pl.pallas_call(
            functools.partial(kernel, ndev, frames),
            out_shape=jax.ShapeDtypeStruct((frames, ndev, SUBL, width), BF),
            in_specs=[pl.BlockSpec(memory_space=pltpu.VMEM)] * 8,
            out_specs=pl.BlockSpec(memory_space=pl.ANY),
            scratch_shapes=[
                pltpu.VMEM((2, width, width), BF),
                pltpu.VMEM((patches, width), BF),
                pltpu.VMEM((patches, width), BF),
                pltpu.VMEM((width, patches), BF),
                pltpu.VMEM((patches, width), BF),
                pltpu.VMEM((2, frames, ndev, SUBL, width), BF),
                pltpu.VMEM((frames, ndev, SUBL, width), BF),
                pltpu.VMEM((frames, SUBL, ndev, width), BF),
                pltpu.VMEM((SUBL, seq, width), BF),
                pltpu.VMEM((SUBL, seq, width), BF),
                pltpu.VMEM((SUBL, width, seq), BF),
                pltpu.VMEM((SUBL, ndev, width), BF),
                pltpu.SemaphoreType.DMA((2, frames)),
                pltpu.SemaphoreType.DMA((2, frames)),
                pltpu.SemaphoreType.DMA((2, frames)),
            ],
            compiler_params=pltpu.CompilerParams(has_side_effects=True, vmem_limit_bytes=67043328),
            name='latte_blocks',
        )(latent[0], ln_gain, ln_bias, wqk, wv, w_out.reshape(2, width, width), w_up, w_down)
        return out.reshape(1, frames, patches, width)

    return jax.shard_map(local_run, mesh=mesh, in_specs=(act_spec, P(), P(), P(), P(), P(), P()), out_specs=act_spec, check_vma=False)
```

time: 528 us -> 408 us (0.77); the launches traced: 520 us -> 407 us
  Pallas kernels: 0 us -> 398 us
  matrix products: 285 us -> 0 us
  blocking collectives: 171 us -> 0 us
  local copies, waits for them, and re-layouts: 46.2 us -> 8.91 us
  other arithmetic: 17.2 us -> 0 us
    pallas_call x0 -> x1, Pallas kernels: none -> 398 us  [local_run(): pl.pallas_call(functools.partial(kernel, ndev, frames), out_shape=jax.Sha...]
    dot_general x8 -> x0, matrix products: 184 us -> none  [the longest x2 89.2 us: attend(): jnp.einsum(ein_forms[1], attn_probs, value_rows, preferred_element_type=j...]
    all_to_all x2 -> x0, blocking collectives: 171 us -> none  [the longest x1 96.9 us: local_run(): mixed_act = lax.all_to_all(mixed_act, 'sp', 2, 1, tiled=True)]
    sub x2 -> x0, matrix products: 101 us -> none  [attend(): attn_probs = jax.nn.softmax(scores, axis=-1).astype(jnp.bfloat16)]
    convert_element_type x5 -> x0, local copies, waits for them, and re-layouts: 32.4 us -> none  [the longest x2 15.5 us: finish_block(): return result.astype(jnp.bfloat16)]
    reduce_sum x6 -> x0, other arithmetic: 13.6 us -> none  [the longest x4 8.81 us: layer_norm(): variance = jnp.mean(centered * centered, axis=-1, keepdims=True)]
    unnamed x35 -> x5, local copies, waits for them, and re-layouts: 11.1 us -> 7.53 us
where the time goes in v1:
time: 408 us; the launch traced here: 407 us
  Pallas kernels  398 us (98%)
  local copies, waits for them, and re-layouts  8.91 us (2%)
    pallas_call x1, Pallas kernels, local_run(): pl.pallas_call(functools.partial(kernel, ndev, frames), out_shape=jax.Sha...  398 us

profile of v1, /device:TPU:1, one launch (start us, length us, event | category | flops | bytes accessed | tf_op | source)
XLA Modules:
  0.0 407.4 jit_solution(14826623577958329140)
XLA Ops:
  0.0 0.0 copy-start
  0.0 1.3 slice.9
  1.3 1.1 copy.12.wv_ref
  2.3 0.0 copy-done
  2.3 0.1 slice.8
  2.5 1.5 copy.11.wqk_ref
  3.9 398.5 %latte_blocks.1 = bf16[6,128,8,384]{3,2,1,0:T(8,128)(2,1)} custom-call(bf16[6,1024,384]{2,1,0:T(8,128)(2,1)} %bitcast.5, bf16[4,384]{1,0:T(4,128)(2,1)} %gain_ref.1, bf16[4,384]{1,0:T(4,128)(2,1)} %shift_ref.1, bf16[2,384,768]{2,1,0:T(8,128)(2,1)} %copy.11.wqk_ref, bf16[2,384,384]{2,1,0:T(8,128)(2,1)} %copy.12.wv_ref, bf16[2,384,384]{2,1,0:T(8,128)(2,1)} %bitcast.8, ...), custom_call_target="tpu_custom_call" | custom-call | tf_op jit(solution)/shard_map/latte_blocks/pallas_call | solution.py:218
  402.4 5.0 %copy.14 = bf16[1,6,1024,384]{3,2,1,0:T(8,128)(2,1)} copy(bf16[1,6,1024,384]{3,2,1,0:T(8,128)(2,1)} %bitcast.4) | data formatting | bytes 9437184
Async XLA Ops:
  0.0 2.3 copy-start

commit v2 on v1

v2 whole, which is shorter than its diff:
```python
import functools
import jax
import jax.numpy as jnp
from jax import lax
from jax.experimental import pallas as pl
from jax.experimental.pallas import tpu as pltpu
from jax.sharding import PartitionSpec as P

LN_EPS = 1e-6
HEADS = 6
HEAD_DIM = 64
BF = jnp.bfloat16
F32 = jnp.float32
SUBL = 8
TILE = 256
PLANES = 4
ORDER = (2, 6, 4, 3, 7, 5, 1)
KEYS = 256
GROUP = 8
CHUNK = 256
HIDDEN = 768
MLPS = 2
EXP2_SCALE = 1.4426950408889634 * HEAD_DIM ** -0.5


def layer_norm(xf, gain, shift):
    mean = jnp.mean(xf, axis=-1, keepdims=True)
    cen = xf - mean
    var = jnp.mean(cen * cen, axis=-1, keepdims=True)
    return (cen * lax.rsqrt(var + LN_EPS) * gain + shift).astype(BF)


def dot(a, b):
    return jnp.dot(a, b, preferred_element_type=F32)


def dot_t(a, b):
    return lax.dot_general(a, b, (((1,), (1,)), ((), ())), preferred_element_type=F32)


def gelu(x):
    inner = x * (0.7978845608028654 + 0.035677408136300125 * (x * x))
    half = 0.5 * x
    return half + half * jnp.tanh(inner)


def score(q, k_at, keys, head, s_ref, m_ref):
    lane = lax.broadcasted_iota(jnp.int32, (TILE, 128), 1)
    qm = jnp.where(lax.div(lane, HEAD_DIM) == head % 2, q, jnp.zeros_like(q))
    slot = head % 2
    top = None
    for c in range(keys // KEYS):
        s = dot_t(k_at(c), qm)
        s_ref[slot, c * KEYS:(c + 1) * KEYS, :] = s
        t = jnp.max(s.reshape(KEYS // GROUP, GROUP, TILE), axis=0)
        top = t if top is None else jnp.maximum(top, t)
        yield
    m_ref[slot] = jnp.broadcast_to(jnp.max(top, axis=0, keepdims=True), (8, TILE))
    yield


def mix(v_at, keys, head, s_ref, m_ref, out):
    slot = head % 2
    top = m_ref[slot, 0:1, :]
    total = None
    o = None
    for c in range(keys // KEYS):
        e = jnp.exp2((s_ref[slot, c * KEYS:(c + 1) * KEYS, :] - top) * EXP2_SCALE)
        t = jnp.sum(e.reshape(KEYS // GROUP, GROUP, TILE), axis=0)
        total = t if total is None else total + t
        d = dot(v_at(c), e.astype(BF))
        o = d if o is None else o + d
        yield
    out.append(o * (1.0 / jnp.sum(total, axis=0, keepdims=True)))
    yield


def together(*steps):
    live = list(steps)
    while live:
        live = [g for g in live if next(g, live) is not live]


def attention(tiles, q_at, k_at, v_at, keys, s_ref, m_ref, put):
    def scores(t, head):
        return score(q_at(t, head // 2), lambda c: k_at(t, head // 2, c), keys, head, s_ref, m_ref)

    together(scores(0, 0))

    def step(t, carry):
        after = lax.rem(t + 1, tiles)
        out = []
        for head in range(HEADS):
            ahead = scores(t, head + 1) if head + 1 < HEADS else scores(after, 0)
            together(ahead, mix(lambda c: v_at(t, head, c), keys, head, s_ref, m_ref, out))
            if head % 2:
                put(t, head // 2, jnp.concatenate(out, axis=0).T.astype(BF))
                out = []
        return carry
    lax.fori_loop(0, tiles, step, 0)


def finish(xb, o, gain, shift, wout, wup, wdown, out):
    h = (xb.astype(F32) + dot(o, wout[...])).astype(BF)
    hf = h.astype(F32)
    yield
    a = layer_norm(hf, gain, shift)
    yield
    y = hf
    hidden = wup.shape[1]
    for c in range(0, hidden, HIDDEN):
        u = gelu(dot(a, wup[:, c:c + HIDDEN])).astype(BF)
        y = y + dot(u, wdown[c:c + HIDDEN, :])
        yield
    out.append(y)
    yield


def kernel(ndev, frames, x_ref, gain_ref, shift_ref, wqkv_ref, wout_ref, wup_ref, wdown_ref, out_ref,
           wqk, qs, ks, vts, os_, sendbuf, recv, xt, q1, k1, v1t, o1, y1, s_scr, m_scr, send_sem, recv_sem, loc_sem):
    patches = ndev * SUBL
    width = HEADS * HEAD_DIM
    seq = frames * ndev
    me = lax.axis_index('sp')
    core, cx = lax.rem(me, 2), lax.rem(lax.div(me, 2), 4)
    cy, cz = lax.rem(lax.div(me, 8), 4), lax.div(me, 32)
    at_x = [lax.rem(cx + d, 4) * 2 for d in range(4)]
    at_core = [lax.rem(core + d, 2) for d in range(2)]
    nchunk = patches // CHUNK

    for l in range(2):
        wqk[l] = wqkv_ref[l, :2 * width, :].astype(F32).T.astype(BF)

    def send_to(stage, dst, j, to):
        pltpu.make_async_remote_copy(
            src_ref=sendbuf.at[stage, j, to], dst_ref=dst.at[j, me],
            send_sem=send_sem.at[stage, j], recv_sem=recv_sem.at[stage, j],
            device_id={'sp': to}, device_id_type=pl.DeviceIdType.MESH).start()

    def plane(g):
        return lax.rem(cz + lax.div(g, 4), 4) * 32 + lax.rem(cy + lax.rem(g, 4), 4) * 8

    def send_round(stage, dst, j):
        pltpu.make_async_copy(sendbuf.at[stage, j, me], dst.at[j, me], loc_sem.at[stage, j]).start()

        def column(g, c):
            send_to(stage, dst, j, plane(g) + at_x[0] + at_core[0])
            return c
        lax.fori_loop(1, ndev // 8, column, 0)

        def planes(i, c):
            for g in range(PLANES):
                base = plane(i * PLANES + g)
                for d in ORDER:
                    send_to(stage, dst, j, base + at_x[d // 2] + at_core[d % 2])
            return c
        lax.fori_loop(0, ndev // 8 // PLANES, planes, 0)

    def wait_bytes(ref, sem):
        pltpu.make_async_copy(ref, ref, sem).wait()

    def wait_arrived(stage, dst, j):
        pltpu.make_async_copy(sendbuf.at[stage, j, 0], dst.at[j, 0], loc_sem.at[stage, j]).wait()
        wait_bytes(dst.at[j, pl.ds(0, ndev - 1)], recv_sem.at[stage, j])

    def wait_sent(stage, j):
        wait_bytes(sendbuf.at[stage, j, pl.ds(0, ndev - 1)], send_sem.at[stage, j])

    def params(l):
        g = gain_ref[...].astype(F32)
        b = shift_ref[...].astype(F32)
        return g[2 * l:2 * l + 1], b[2 * l:2 * l + 1], g[2 * l + 1:2 * l + 2], b[2 * l + 1:2 * l + 2]

    ga, ba, gm, bm = params(0)

    def frame_step(j, carry):
        def qkv_step(c, cc):
            rows = pl.ds(pl.multiple_of(c * CHUNK, CHUNK), CHUNK)
            a = layer_norm(x_ref[j, rows, :].astype(F32), ga, ba)
            qk = dot(a, wqk[0]).astype(BF)
            qs[rows, :] = qk[:, :width]
            ks[rows, :] = qk[:, width:]
            vts[:, rows] = dot_t(wqkv_ref[0, 2 * width:, :], a).astype(BF)
            return cc
        lax.fori_loop(0, nchunk, qkv_step, 0)

        def put(t, pair, o):
            os_[pl.ds(pl.multiple_of(t * TILE, TILE), TILE), 128 * pair:128 * pair + 128] = o
        attention(
            patches // TILE,
            lambda t, p: qs[pl.ds(pl.multiple_of(t * TILE, TILE), TILE), 128 * p:128 * p + 128],
            lambda t, p, c: ks[c * KEYS:(c + 1) * KEYS, 128 * p:128 * p + 128],
            lambda t, h, c: vts[HEAD_DIM * h:HEAD_DIM * h + HEAD_DIM, c * KEYS:(c + 1) * KEYS],
            patches, s_scr, m_scr, put)

        def mlp_step(c, cc):
            outs = [[] for _ in range(MLPS)]
            rows = [pl.ds(pl.multiple_of((c * MLPS + i) * CHUNK, CHUNK), CHUNK) for i in range(MLPS)]
            together(*[finish(x_ref[j, r, :], os_[r, :], gm, bm, wout_ref.at[0], wup_ref.at[0], wdown_ref.at[0], out)
                       for r, out in zip(rows, outs)])
            dests = CHUNK // SUBL
            for i in range(MLPS):
                to = pl.ds(pl.multiple_of((c * MLPS + i) * dests, dests), dests)
                sendbuf[0, j, to] = outs[i][0].reshape(dests, SUBL, width).astype(BF)
            return cc
        lax.fori_loop(0, nchunk // MLPS, mlp_step, 0)
        send_round(0, recv, j)
        return carry

    lax.fori_loop(0, frames, frame_step, 0)

    ga, ba, gm, bm = params(1)
    r_io = lax.broadcasted_iota(jnp.int32, (128, 128), 0)
    c_io = lax.broadcasted_iota(jnp.int32, (128, 128), 1)
    to_seq = jnp.where((r_io // 16 == c_io % 8) & (r_io % 16 == c_io // 8), 1.0, 0.0).astype(BF)
    to_tok = jnp.where((r_io % 8 == c_io // 16) & (r_io // 8 == c_io % 16), 1.0, 0.0).astype(BF)

    def kv_step(j, carry):
        wait_arrived(0, recv, j)

        def perm_step(g, cc):
            blk = recv[j, pl.ds(g * 16, 16)].astype(F32).reshape(128, width).astype(BF)
            seqd = dot(to_seq, blk).astype(BF)
            for p in range(SUBL):
                xt[j, p, pl.ds(pl.multiple_of(g * 16, 16), 16), :] = seqd[16 * p:16 * p + 16]
            return cc
        lax.fori_loop(0, ndev // 16, perm_step, 0)

        def qkv_step(c, cc):
            xb = xt[j, pl.ds(2 * c, 2)].reshape(2 * ndev, width)
            a = layer_norm(xb.astype(F32), ga, ba)
            qk = dot(a, wqk[1]).astype(BF)
            vt = dot_t(wqkv_ref[1, 2 * width:, :], a).astype(BF)
            cols = pl.ds(pl.multiple_of(j * ndev, ndev), ndev)
            for i in range(2):
                part = slice(i * ndev, (i + 1) * ndev)
                q1[2 * c + i, cols, :] = qk[part, :width]
                k1[2 * c + i, cols, :] = qk[part, width:]
                v1t[2 * c + i, :, cols] = vt[:, part]
            return cc
        lax.fori_loop(0, SUBL // 2, qkv_step, 0)
        return carry
    lax.fori_loop(0, frames, kv_step, 0)

    def time_step(jj, carry):
        first = pl.multiple_of(jj * TILE, TILE)

        def put(p, pair, o):
            o1[p, :, 128 * pair:128 * pair + 128] = o
        attention(
            SUBL,
            lambda t, p: q1[t, pl.ds(first, TILE), 128 * p:128 * p + 128],
            lambda t, p, c: k1[t, c * KEYS:(c + 1) * KEYS, 128 * p:128 * p + 128],
            lambda t, h, c: v1t[t, HEAD_DIM * h:HEAD_DIM * h + HEAD_DIM, c * KEYS:(c + 1) * KEYS],
            seq, s_scr, m_scr, put)

        def half_step(half, carry):
            j = jj * (TILE // ndev) + half
            part = pl.ds(pl.multiple_of(half * ndev, ndev), ndev)

            def mlp_step(c, cc):
                outs = [[] for _ in range(MLPS)]
                at = [pl.ds((c * MLPS + i) * 2, 2) for i in range(MLPS)]
                together(*[finish(xt[j, r].reshape(CHUNK, width), o1[r, part, :].reshape(CHUNK, width), gm, bm,
                                  wout_ref.at[1], wup_ref.at[1], wdown_ref.at[1], out) for r, out in zip(at, outs)])
                for i in range(MLPS):
                    y1[at[i]] = outs[i][0].astype(BF).reshape(2, ndev, width)
                return cc
            lax.fori_loop(0, SUBL // 2 // MLPS, mlp_step, 0)

            def perm_step(g, cc):
                blk = y1[:, pl.ds(pl.multiple_of(g * 16, 16), 16), :].reshape(128, width)
                tok = dot(to_tok, blk)
                sendbuf[1, j, pl.ds(g * 16, 16)] = tok.reshape(16, SUBL, width).astype(BF)
                return cc
            lax.fori_loop(0, ndev // 16, perm_step, 0)
            send_round(1, out_ref, j)
            return carry
        lax.fori_loop(0, TILE // ndev, half_step, 0)
        return carry

    lax.fori_loop(0, seq // TILE, time_step, 0)

    def drain(j, carry):
        wait_sent(0, j)
        wait_sent(1, j)
        wait_arrived(1, out_ref, j)
        return carry
    lax.fori_loop(0, frames, drain, 0)


def solution(mesh):
    ndev = mesh.shape['sp']
    act_spec = P('data', 'sp', None, None)

    def local_run(latent, ln_gain, ln_bias, w_qkv, w_out, w_up, w_down):
        _, frames, patches, width = latent.shape
        wqkv_t = w_qkv.transpose(0, 2, 3, 4, 1).reshape(2, 3 * width, width)
        seq = frames * ndev
        out = pl.pallas_call(
            functools.partial(kernel, ndev, frames),
            out_shape=jax.ShapeDtypeStruct((frames, ndev, SUBL, width), BF),
            in_specs=[pl.BlockSpec(memory_space=pltpu.VMEM)] * 7,
            out_specs=pl.BlockSpec(memory_space=pl.ANY),
            scratch_shapes=[
                pltpu.VMEM((2, width, 2 * width), BF),
                pltpu.VMEM((patches, width), BF),
                pltpu.VMEM((patches, width), BF),
                pltpu.VMEM((width, patches), BF),
                pltpu.VMEM((patches, width), BF),
                pltpu.VMEM((2, frames, ndev, SUBL, width), BF),
                pltpu.VMEM((frames, ndev, SUBL, width), BF),
                pltpu.VMEM((frames, SUBL, ndev, width), BF),
                pltpu.VMEM((SUBL, seq, width), BF),
                pltpu.VMEM((SUBL, seq, width), BF),
                pltpu.VMEM((SUBL, width, seq), BF),
                pltpu.VMEM((SUBL, 2 * ndev, width), BF),
                pltpu.VMEM((SUBL, ndev, width), BF),
                pltpu.VMEM((2, max(patches, seq), TILE), F32),
                pltpu.VMEM((2, 8, TILE), F32),
                pltpu.SemaphoreType.DMA((2, frames)),
                pltpu.SemaphoreType.DMA((2, frames)),
                pltpu.SemaphoreType.DMA((2, frames)),
            ],
            compiler_params=pltpu.CompilerParams(has_side_effects=True, vmem_limit_bytes=67043328),
            name='latte_blocks',
        )(latent[0], ln_gain, ln_bias, wqkv_t, w_out.reshape(2, width, width), w_up, w_down)
        return out.reshape(1, frames, patches, width)

    return jax.shard_map(local_run, mesh=mesh, in_specs=(act_spec, P(), P(), P(), P(), P(), P()), out_specs=act_spec, check_vma=False)
```

time: 408 us -> 240 us (0.59)
  Pallas kernels: 398 us -> 235 us
    pallas_call x1, Pallas kernels: 398 us -> 235 us  [local_run(): pl.pallas_call(functools.partial(kernel, ndev, frames), out_shape=jax.Sha...]
where the time goes in v2:
time: 240 us
  Pallas kernels  235 us (98%)
  local copies, waits for them, and re-layouts  5 us (2%)
    pallas_call x1, Pallas kernels, local_run(): pl.pallas_call(functools.partial(kernel, ndev, frames), out_shape=jax.Sha...  235 us
    unnamed x1, local copies, waits for them, and re-layouts  5 us

profile of v2, /device:TPU:1, one launch (start us, length us, event | category | flops | bytes accessed | tf_op | source)
XLA Modules:
  0.0 240.0 jit_solution(4998334419314858305)
XLA Ops:
  0.0 235.0 %latte_blocks.1 = bf16[6,128,8,384]{3,2,1,0:T(8,128)(2,1)} custom-call(bf16[6,1024,384]{2,1,0:T(8,128)(2,1)} %bitcast.7, bf16[4,384]{1,0:T(4,128)(2,1)} %gain_ref.1, bf16[4,384]{1,0:T(4,128)(2,1)} %shift_ref.1, bf16[2,1152,384]{2,1,0:T(8,128)(2,1)} %bitcast.8, bf16[2,384,384]{2,1,0:T(8,128)(2,1)} %bitcast.9, bf16[2,384,1536]{2,1,0:T(8,128)(2,1)} %wup_ref.1, ...), custom_call_target="tpu_custom_call" | custom-call | tf_op jit(solution)/shard_map/latte_blocks/pallas_call | solution.py:300
  235.0 5.0 %copy.9 = bf16[1,6,1024,384]{3,2,1,0:T(8,128)(2,1)} copy(bf16[1,6,1024,384]{3,2,1,0:T(8,128)(2,1)} %bitcast.6) | data formatting | bytes 9437184

commit v3 on v2

--- a/solution.py
+++ b/solution.py
@@ -13,13 +13,15 @@
 F32 = jnp.float32
 SUBL = 8
 TILE = 256
-PLANES = 4
+OFFSETS = [o for o in (i * 37 % 128 for i in range(1, 128))]
+PERMS = 8
+QKVS = 4
 ORDER = (2, 6, 4, 3, 7, 5, 1)
-KEYS = 256
+STEPS = 2
 GROUP = 8
 CHUNK = 256
 HIDDEN = 768
-MLPS = 2
+MLPS = 4
 EXP2_SCALE = 1.4426950408889634 * HEAD_DIM ** -0.5
 
 
@@ -49,10 +51,11 @@
     qm = jnp.where(lax.div(lane, HEAD_DIM) == head % 2, q, jnp.zeros_like(q))
     slot = head % 2
     top = None
-    for c in range(keys // KEYS):
+    step = keys // STEPS
+    for c in range(STEPS):
         s = dot_t(k_at(c), qm)
-        s_ref[slot, c * KEYS:(c + 1) * KEYS, :] = s
-        t = jnp.max(s.reshape(KEYS // GROUP, GROUP, TILE), axis=0)
+        s_ref[slot, c * step:(c + 1) * step, :] = s
+        t = jnp.max(s.reshape(step // GROUP, GROUP, TILE), axis=0)
         top = t if top is None else jnp.maximum(top, t)
         yield
     m_ref[slot] = jnp.broadcast_to(jnp.max(top, axis=0, keepdims=True), (8, TILE))
@@ -64,9 +67,10 @@
     top = m_ref[slot, 0:1, :]
     total = None
     o = None
-    for c in range(keys // KEYS):
-        e = jnp.exp2((s_ref[slot, c * KEYS:(c + 1) * KEYS, :] - top) * EXP2_SCALE)
-        t = jnp.sum(e.reshape(KEYS // GROUP, GROUP, TILE), axis=0)
+    step = keys // STEPS
+    for c in range(STEPS):
+        e = jnp.exp2((s_ref[slot, c * step:(c + 1) * step, :] - top) * EXP2_SCALE)
+        t = jnp.sum(e.reshape(step // GROUP, GROUP, TILE), axis=0)
         total = t if total is None else total + t
         d = dot(v_at(c), e.astype(BF))
         o = d if o is None else o + d
@@ -116,6 +120,15 @@
     yield
 
 
+def project(xb, gain, shift, wqk, wvt, put):
+    a = layer_norm(xb.astype(F32), gain, shift)
+    yield
+    qk = dot(a, wqk[...]).astype(BF)
+    yield
+    put(qk, dot_t(wvt[...], a).astype(BF))
+    yield
+
+
 def kernel(ndev, frames, x_ref, gain_ref, shift_ref, wqkv_ref, wout_ref, wup_ref, wdown_ref, out_ref,
            wqk, qs, ks, vts, os_, sendbuf, recv, xt, q1, k1, v1t, o1, y1, s_scr, m_scr, send_sem, recv_sem, loc_sem):
     patches = ndev * SUBL
@@ -124,6 +137,8 @@
     me = lax.axis_index('sp')
     core, cx = lax.rem(me, 2), lax.rem(lax.div(me, 2), 4)
     cy, cz = lax.rem(lax.div(me, 8), 4), lax.div(me, 32)
+    at_z = [lax.rem(cz + d, 4) * 32 for d in range(4)]
+    at_y = [lax.rem(cy + d, 4) * 8 for d in range(4)]
     at_x = [lax.rem(cx + d, 4) * 2 for d in range(4)]
     at_core = [lax.rem(core + d, 2) for d in range(2)]
     nchunk = patches // CHUNK
@@ -137,24 +152,10 @@
             send_sem=send_sem.at[stage, j], recv_sem=recv_sem.at[stage, j],
             device_id={'sp': to}, device_id_type=pl.DeviceIdType.MESH).start()
 
-    def plane(g):
-        return lax.rem(cz + lax.div(g, 4), 4) * 32 + lax.rem(cy + lax.rem(g, 4), 4) * 8
-
     def send_round(stage, dst, j):
         pltpu.make_async_copy(sendbuf.at[stage, j, me], dst.at[j, me], loc_sem.at[stage, j]).start()
-
-        def column(g, c):
-            send_to(stage, dst, j, plane(g) + at_x[0] + at_core[0])
-            return c
-        lax.fori_loop(1, ndev // 8, column, 0)
-
-        def planes(i, c):
-            for g in range(PLANES):
-                base = plane(i * PLANES + g)
-                for d in ORDER:
-                    send_to(stage, dst, j, base + at_x[d // 2] + at_core[d % 2])
-            return c
-        lax.fori_loop(0, ndev // 8 // PLANES, planes, 0)
+        for d in OFFSETS:
+            send_to(stage, dst, j, at_z[d // 32] + at_y[d // 8 % 4] + at_x[d // 2 % 4] + at_core[d % 2])
 
     def wait_bytes(ref, sem):
         pltpu.make_async_copy(ref, ref, sem).wait()
@@ -175,22 +176,24 @@
 
     def frame_step(j, carry):
         def qkv_step(c, cc):
-            rows = pl.ds(pl.multiple_of(c * CHUNK, CHUNK), CHUNK)
-            a = layer_norm(x_ref[j, rows, :].astype(F32), ga, ba)
-            qk = dot(a, wqk[0]).astype(BF)
-            qs[rows, :] = qk[:, :width]
-            ks[rows, :] = qk[:, width:]
-            vts[:, rows] = dot_t(wqkv_ref[0, 2 * width:, :], a).astype(BF)
+            def put_at(rows):
+                def put(qk, vt):
+                    qs[rows, :] = qk[:, :width]
+                    ks[rows, :] = qk[:, width:]
+                    vts[:, rows] = vt
+                return put
+            rows = [pl.ds(pl.multiple_of((c * QKVS + i) * CHUNK, CHUNK), CHUNK) for i in range(QKVS)]
+            together(*[project(x_ref[j, r, :], ga, ba, wqk.at[0], wqkv_ref.at[0, 2 * width:, :], put_at(r)) for r in rows])
             return cc
-        lax.fori_loop(0, nchunk, qkv_step, 0)
+        lax.fori_loop(0, nchunk // QKVS, qkv_step, 0)
 
         def put(t, pair, o):
             os_[pl.ds(pl.multiple_of(t * TILE, TILE), TILE), 128 * pair:128 * pair + 128] = o
         attention(
             patches // TILE,
             lambda t, p: qs[pl.ds(pl.multiple_of(t * TILE, TILE), TILE), 128 * p:128 * p + 128],
-            lambda t, p, c: ks[c * KEYS:(c + 1) * KEYS, 128 * p:128 * p + 128],
-            lambda t, h, c: vts[HEAD_DIM * h:HEAD_DIM * h + HEAD_DIM, c * KEYS:(c + 1) * KEYS],
+            lambda t, p, c: ks[c * (patches // STEPS):(c + 1) * (patches // STEPS), 128 * p:128 * p + 128],
+            lambda t, h, c: vts[HEAD_DIM * h:HEAD_DIM * h + HEAD_DIM, c * (patches // STEPS):(c + 1) * (patches // STEPS)],
             patches, s_scr, m_scr, put)
 
         def mlp_step(c, cc):
@@ -218,27 +221,32 @@
     def kv_step(j, carry):
         wait_arrived(0, recv, j)
 
-        def perm_step(g, cc):
-            blk = recv[j, pl.ds(g * 16, 16)].astype(F32).reshape(128, width).astype(BF)
-            seqd = dot(to_seq, blk).astype(BF)
-            for p in range(SUBL):
-                xt[j, p, pl.ds(pl.multiple_of(g * 16, 16), 16), :] = seqd[16 * p:16 * p + 16]
+        def perm_step(i, cc):
+            for k in range(PERMS):
+                g = i * PERMS + k
+                blk = recv[j, pl.ds(g * 16, 16)].astype(F32).reshape(128, width).astype(BF)
+                seqd = dot(to_seq, blk).astype(BF)
+                for p in range(SUBL):
+                    xt[j, p, pl.ds(pl.multiple_of(g * 16, 16), 16), :] = seqd[16 * p:16 * p + 16]
             return cc
-        lax.fori_loop(0, ndev // 16, perm_step, 0)
+        lax.fori_loop(0, ndev // 16 // PERMS, perm_step, 0)
 
         def qkv_step(c, cc):
-            xb = xt[j, pl.ds(2 * c, 2)].reshape(2 * ndev, width)
-            a = layer_norm(xb.astype(F32), ga, ba)
-            qk = dot(a, wqk[1]).astype(BF)
-            vt = dot_t(wqkv_ref[1, 2 * width:, :], a).astype(BF)
             cols = pl.ds(pl.multiple_of(j * ndev, ndev), ndev)
-            for i in range(2):
-                part = slice(i * ndev, (i + 1) * ndev)
-                q1[2 * c + i, cols, :] = qk[part, :width]
-                k1[2 * c + i, cols, :] = qk[part, width:]
-                v1t[2 * c + i, :, cols] = vt[:, part]
+
+            def put_at(first):
+                def put(qk, vt):
+                    for i in range(2):
+                        part = slice(i * ndev, (i + 1) * ndev)
+                        q1[first + i, cols, :] = qk[part, :width]
+                        k1[first + i, cols, :] = qk[part, width:]
+                        v1t[first + i, :, cols] = vt[:, part]
+                return put
+            firsts = [(c * QKVS + i) * 2 for i in range(QKVS)]
+            together(*[project(xt[j, pl.ds(f, 2)].reshape(2 * ndev, width), ga, ba, wqk.at[1], wqkv_ref.at[1, 2 * width:, :], put_at(f))
+                       for f in firsts])
             return cc
-        lax.fori_loop(0, SUBL // 2, qkv_step, 0)
+        lax.fori_loop(0, SUBL // 2 // QKVS, qkv_step, 0)
         return carry
     lax.fori_loop(0, frames, kv_step, 0)
 
@@ -250,8 +258,8 @@
         attention(
             SUBL,
             lambda t, p: q1[t, pl.ds(first, TILE), 128 * p:128 * p + 128],
-            lambda t, p, c: k1[t, c * KEYS:(c + 1) * KEYS, 128 * p:128 * p + 128],
-            lambda t, h, c: v1t[t, HEAD_DIM * h:HEAD_DIM * h + HEAD_DIM, c * KEYS:(c + 1) * KEYS],
+            lambda t, p, c: k1[t, c * (seq // STEPS):(c + 1) * (seq // STEPS), 128 * p:128 * p + 128],
+            lambda t, h, c: v1t[t, HEAD_DIM * h:HEAD_DIM * h + HEAD_DIM, c * (seq // STEPS):(c + 1) * (seq // STEPS)],
             seq, s_scr, m_scr, put)
 
         def half_step(half, carry):
@@ -268,12 +276,14 @@
                 return cc
             lax.fori_loop(0, SUBL // 2 // MLPS, mlp_step, 0)
 
-            def perm_step(g, cc):
-                blk = y1[:, pl.ds(pl.multiple_of(g * 16, 16), 16), :].reshape(128, width)
-                tok = dot(to_tok, blk)
-                sendbuf[1, j, pl.ds(g * 16, 16)] = tok.reshape(16, SUBL, width).astype(BF)
+            def perm_step(i, cc):
+                for k in range(PERMS):
+                    g = i * PERMS + k
+                    blk = y1[:, pl.ds(pl.multiple_of(g * 16, 16), 16), :].reshape(128, width)
+                    tok = dot(to_tok, blk)
+                    sendbuf[1, j, pl.ds(g * 16, 16)] = tok.reshape(16, SUBL, width).astype(BF)
                 return cc
-            lax.fori_loop(0, ndev // 16, perm_step, 0)
+            lax.fori_loop(0, ndev // 16 // PERMS, perm_step, 0)
             send_round(1, out_ref, j)
             return carry
         lax.fori_loop(0, TILE // ndev, half_step, 0)

time: 240 us -> 205 us (0.85)
  Pallas kernels: 235 us -> 200 us
    pallas_call x1, Pallas kernels: 235 us -> 200 us  [local_run(): pl.pallas_call(functools.partial(kernel, ndev, frames), out_shape=jax.Sha...]
where the time goes in v3:
time: 205 us
  Pallas kernels  200 us (98%)
  local copies, waits for them, and re-layouts  5 us (2%)
    pallas_call x1, Pallas kernels, local_run(): pl.pallas_call(functools.partial(kernel, ndev, frames), out_shape=jax.Sha...  200 us
    unnamed x1, local copies, waits for them, and re-layouts  5 us

profile of v3, /device:TPU:1, one launch (start us, length us, event | category | flops | bytes accessed | tf_op | source)
XLA Modules:
  0.0 204.7 jit_solution(17206710759697165444)
XLA Ops:
  0.0 199.7 %latte_blocks.1 = bf16[6,128,8,384]{3,2,1,0:T(8,128)(2,1)} custom-call(bf16[6,1024,384]{2,1,0:T(8,128)(2,1)} %bitcast.7, bf16[4,384]{1,0:T(4,128)(2,1)} %gain_ref.1, bf16[4,384]{1,0:T(4,128)(2,1)} %shift_ref.1, bf16[2,1152,384]{2,1,0:T(8,128)(2,1)} %bitcast.8, bf16[2,384,384]{2,1,0:T(8,128)(2,1)} %bitcast.9, bf16[2,384,1536]{2,1,0:T(8,128)(2,1)} %wup_ref.1, ...), custom_call_target="tpu_custom_call" | custom-call | tf_op jit(solution)/shard_map/latte_blocks/pallas_call | solution.py:310
  199.7 5.0 %copy.9 = bf16[1,6,1024,384]{3,2,1,0:T(8,128)(2,1)} copy(bf16[1,6,1024,384]{3,2,1,0:T(8,128)(2,1)} %bitcast.6) | data formatting | bytes 9437184

commit v4 on v3

--- a/solution.py
+++ b/solution.py
@@ -15,6 +15,7 @@
 TILE = 256
 OFFSETS = [o for o in (i * 37 % 128 for i in range(1, 128))]
 PERMS = 8
+TILES = 4
 QKVS = 4
 ORDER = (2, 6, 4, 3, 7, 5, 1)
 STEPS = 2
@@ -49,7 +50,7 @@
 def score(q, k_at, keys, head, s_ref, m_ref):
     lane = lax.broadcasted_iota(jnp.int32, (TILE, 128), 1)
     qm = jnp.where(lax.div(lane, HEAD_DIM) == head % 2, q, jnp.zeros_like(q))
-    slot = head % 2
+    slot = head
     top = None
     step = keys // STEPS
     for c in range(STEPS):
@@ -63,7 +64,7 @@
 
 
 def mix(v_at, keys, head, s_ref, m_ref, out):
-    slot = head % 2
+    slot = head
     top = m_ref[slot, 0:1, :]
     total = None
     o = None
@@ -89,19 +90,22 @@
     def scores(t, head):
         return score(q_at(t, head // 2), lambda c: k_at(t, head // 2, c), keys, head, s_ref, m_ref)
 
-    together(scores(0, 0))
-
-    def step(t, carry):
-        after = lax.rem(t + 1, tiles)
-        out = []
-        for head in range(HEADS):
-            ahead = scores(t, head + 1) if head + 1 < HEADS else scores(after, 0)
-            together(ahead, mix(lambda c: v_at(t, head, c), keys, head, s_ref, m_ref, out))
-            if head % 2:
-                put(t, head // 2, jnp.concatenate(out, axis=0).T.astype(BF))
-                out = []
-        return carry
-    lax.fori_loop(0, tiles, step, 0)
+    together(scores(0, 0), scores(0, 1))
+
+    def tile(t, after):
+        for head in range(0, HEADS, 2):
+            heads = (head, head + 1)
+            ahead = [scores(t, h + 2) if head + 2 < HEADS else scores(after, h + 2 - HEADS) for h in heads]
+            outs = [[], []]
+            together(*ahead, *[mix(lambda c, h=h: v_at(t, h, c), keys, h, s_ref, m_ref, out) for h, out in zip(heads, outs)])
+            put(t, head // 2, jnp.concatenate([out[0] for out in outs], axis=0).T.astype(BF))
+
+    def step(i, carry):
+        for k in range(TILES):
+            t = i * TILES + k
+            tile(t, t + 1 if k + 1 < TILES else lax.rem(t + 1, tiles))
+        return carry
+    lax.fori_loop(0, tiles // TILES, step, 0)
 
 
 def finish(xb, o, gain, shift, wout, wup, wdown, out):
@@ -129,7 +133,8 @@
     yield
 
 
-def kernel(ndev, frames, x_ref, gain_ref, shift_ref, wqkv_ref, wout_ref, wup_ref, wdown_ref, out_ref,
+def kernel(ndev, frames, x_hbm, gain_ref, shift_ref, wqkv_hbm, wout_hbm, wup_hbm, wdown_hbm, out_ref,
+           x_ref, wqkv_ref, wout_ref, wup_ref, wdown_ref, x_sem, w_sem,
            wqk, qs, ks, vts, os_, sendbuf, recv, xt, q1, k1, v1t, o1, y1, s_scr, m_scr, send_sem, recv_sem, loc_sem):
     patches = ndev * SUBL
     width = HEADS * HEAD_DIM
@@ -143,8 +148,28 @@
     at_core = [lax.rem(core + d, 2) for d in range(2)]
     nchunk = patches // CHUNK
 
-    for l in range(2):
+    weights = ((wqkv_hbm, wqkv_ref), (wout_hbm, wout_ref), (wup_hbm, wup_ref), (wdown_hbm, wdown_ref))
+
+    def load_frame(j):
+        return pltpu.make_async_copy(x_hbm.at[j], x_ref.at[j], x_sem.at[j])
+
+    def load_weights(l):
+        return [pltpu.make_async_copy(src.at[l], dst.at[l], w_sem.at[l, i]) for i, (src, dst) in enumerate(weights)]
+
+    def start_weights(l):
+        for copy in load_weights(l):
+            copy.start()
+
+    def wait_weights(l):
+        for copy in load_weights(l):
+            copy.wait()
         wqk[l] = wqkv_ref[l, :2 * width, :].astype(F32).T.astype(BF)
+
+    start_weights(0)
+    for j in range(frames):
+        load_frame(j).start()
+    start_weights(1)
+    wait_weights(0)
 
     def send_to(stage, dst, j, to):
         pltpu.make_async_remote_copy(
@@ -175,6 +200,8 @@
     ga, ba, gm, bm = params(0)
 
     def frame_step(j, carry):
+        load_frame(j).wait()
+
         def qkv_step(c, cc):
             def put_at(rows):
                 def put(qk, vt):
@@ -211,6 +238,7 @@
         return carry
 
     lax.fori_loop(0, frames, frame_step, 0)
+    wait_weights(1)
 
     ga, ba, gm, bm = params(1)
     r_io = lax.broadcasted_iota(jnp.int32, (128, 128), 0)
@@ -307,12 +335,21 @@
         _, frames, patches, width = latent.shape
         wqkv_t = w_qkv.transpose(0, 2, 3, 4, 1).reshape(2, 3 * width, width)
         seq = frames * ndev
+        any_spec, vmem_spec = pl.BlockSpec(memory_space=pl.ANY), pl.BlockSpec(memory_space=pltpu.VMEM)
+        hidden = w_up.shape[2]
         out = pl.pallas_call(
             functools.partial(kernel, ndev, frames),
             out_shape=jax.ShapeDtypeStruct((frames, ndev, SUBL, width), BF),
-            in_specs=[pl.BlockSpec(memory_space=pltpu.VMEM)] * 7,
+            in_specs=[any_spec, vmem_spec, vmem_spec] + [any_spec] * 4,
             out_specs=pl.BlockSpec(memory_space=pl.ANY),
             scratch_shapes=[
+                pltpu.VMEM((frames, patches, width), BF),
+                pltpu.VMEM((2, 3 * width, width), BF),
+                pltpu.VMEM((2, width, width), BF),
+                pltpu.VMEM((2, width, hidden), BF),
+                pltpu.VMEM((2, hidden, width), BF),
+                pltpu.SemaphoreType.DMA((frames,)),
+                pltpu.SemaphoreType.DMA((2, 4)),
                 pltpu.VMEM((2, width, 2 * width), BF),
                 pltpu.VMEM((patches, width), BF),
                 pltpu.VMEM((patches, width), BF),
@@ -326,8 +363,8 @@
                 pltpu.VMEM((SUBL, width, seq), BF),
                 pltpu.VMEM((SUBL, 2 * ndev, width), BF),
                 pltpu.VMEM((SUBL, ndev, width), BF),
-                pltpu.VMEM((2, max(patches, seq), TILE), F32),
-                pltpu.VMEM((2, 8, TILE), F32),
+                pltpu.VMEM((HEADS, max(patches, seq), TILE), F32),
+                pltpu.VMEM((HEADS, 8, TILE), F32),
                 pltpu.SemaphoreType.DMA((2, frames)),
                 pltpu.SemaphoreType.DMA((2, frames)),
                 pltpu.SemaphoreType.DMA((2, frames)),

time: 205 us -> 195 us (0.951)
  Pallas kernels: 200 us -> 190 us
    pallas_call x1, Pallas kernels: 200 us -> 190 us  [local_run(): pl.pallas_call(functools.partial(kernel, ndev, frames), out_shape=jax.Sha...]
where the time goes in v4:
time: 195 us
  Pallas kernels  190 us (97%)
  local copies, waits for them, and re-layouts  5 us (3%)
    pallas_call x1, Pallas kernels, local_run(): pl.pallas_call(functools.partial(kernel, ndev, frames), out_shape=jax.Sha...  190 us
    unnamed x1, local copies, waits for them, and re-layouts  5 us

profile of v4, /device:TPU:1, one launch (start us, length us, event | category | flops | bytes accessed | tf_op | source)
XLA Modules:
  0.0 194.9 jit_solution(10342919107327911219)
XLA Ops:
  0.0 189.9 %latte_blocks.1 = bf16[6,128,8,384]{3,2,1,0:T(8,128)(2,1)} custom-call(bf16[6,1024,384]{2,1,0:T(8,128)(2,1)} %bitcast.7, bf16[4,384]{1,0:T(4,128)(2,1)} %gain_ref.1, bf16[4,384]{1,0:T(4,128)(2,1)} %shift_ref.1, bf16[2,1152,384]{2,1,0:T(8,128)(2,1)} %bitcast.8, bf16[2,384,384]{2,1,0:T(8,128)(2,1)} %bitcast.9, bf16[2,384,1536]{2,1,0:T(8,128)(2,1)} %wup_hbm.1, ...), custom_call_target="tpu_custom_call" | custom-call | tf_op jit(solution)/shard_map/latte_blocks/pallas_call | solution.py:340
  189.9 5.0 %copy.9 = bf16[1,6,1024,384]{3,2,1,0:T(8,128)(2,1)} copy(bf16[1,6,1024,384]{3,2,1,0:T(8,128)(2,1)} %bitcast.6) | data formatting | bytes 9437184
